TPU v7x, 32 devices: a whole 2x2x4 slice. The times are simulated.
32 devices in a mesh: vpair: 4 (over y, x), rank: 8 (over z, core).
Axes of the slice: x: 2, y: 2, z: 4, core: 2. Of those that a mesh axis runs over, the one named last changes fastest.
Arguments:
- amplitudes: bfloat16 [8, 1200, 1200], P(None, 'vpair', 'rank'), may hold values from -6 to 6
- factors: bfloat16 [1200, 8192], P('vpair', 'rank'), may hold values from -0.1875 to 0.1875
- kernel: bfloat16 [8192, 8192], P('vpair', 'rank'), may hold values from -0.875 to 0.875
- other_terms: float32 [8, 1200, 1200], P(None, 'vpair'), may hold values from -6 to 6
- virt_energy: float32 [1200], replicated, may hold values from 0.2 to 4
- pair_energy: float32 [8], replicated, may hold values from -3 to -0.5
Outputs:
- residual: float32 [8, 1200, 1200], P(None, 'vpair')
- update_rms: float32 [], replicated
All inputs are finite; a program needn't handle non-finite values.
Results may differ from a plain program's by a relative error of at most 0.0035.
Values may be sent and summed in bfloat16 or wider, within the bound.
A program may use at most 192 MiB of HBM per device.

v0:
```python
import jax
import jax.numpy as jnp
from jax import lax
from jax.sharding import PartitionSpec as P

epsilon = 1e-06


def shards(amplitudes, factors, kernel, other_terms, virt_energy, pair_energy):
    vpair_count = lax.axis_size("vpair")
    pair_count = amplitudes.shape[0]
    row_block = amplitudes.shape[1]
    col_block = amplitudes.shape[2]
    virt_count = row_block * vpair_count
    right_block = kernel.shape[1]
    factor_rows = lax.all_gather(factors, "rank", axis=1, tiled=True)
    factor_full = lax.all_gather(factor_rows, "vpair", axis=0, tiled=True)
    factor_cols = lax.dynamic_slice_in_dim(
        factor_full, lax.axis_index("rank") * right_block, right_block, 1
    )
    half_done = jnp.einsum(
        "ons,sh->onh",
        lax.all_gather(amplitudes, "rank", axis=2, tiled=True),
        factor_cols,
        preferred_element_type=jnp.float32,
    ).astype(jnp.bfloat16)
    kernel_sub = lax.all_to_all(kernel, "vpair", split_axis=1, concat_axis=0, tiled=True).astype(
        jnp.float32
    )
    coupled = jnp.einsum(
        "cp,icq->ipq",
        factor_full,
        lax.all_to_all(half_done, "vpair", split_axis=2, concat_axis=1, tiled=True),
        preferred_element_type=jnp.float32,
    )
    weighted = (kernel_sub[None] * coupled).astype(jnp.bfloat16)
    ladder_half = jnp.einsum(
        "ap,ipq->iaq", factor_full, weighted, preferred_element_type=jnp.float32
    ).astype(jnp.bfloat16)
    back_half = lax.all_to_all(ladder_half, "vpair", split_axis=1, concat_axis=2, tiled=True)
    partial_value = jnp.einsum(
        "iaq,bq->iab", back_half, factor_cols, preferred_element_type=jnp.float32
    )
    row_energy = lax.dynamic_slice_in_dim(
        virt_energy, lax.axis_index("vpair") * row_block, row_block, 0
    )
    ladder_share = lax.psum_scatter(partial_value, "rank", scatter_dimension=2, tiled=True)
    col_start = lax.axis_index("rank") * col_block
    own_terms = lax.dynamic_slice_in_dim(other_terms, col_start, col_block, 2)
    part_residual = own_terms + ladder_share
    col_energy = lax.dynamic_slice_in_dim(virt_energy, col_start, col_block, 0)
    denominator = row_energy[None, :, None] + col_energy[None, None, :] - pair_energy[:, None, None]
    update = part_residual / denominator
    squares = lax.psum(jnp.sum(update * update), ("vpair", "rank"))
    residual = lax.all_gather(part_residual, "rank", axis=2, tiled=True)
    update_rms = jnp.sqrt(squares / (pair_count * virt_count * virt_count) + epsilon)
    return (residual, update_rms)


def solution(mesh):
    placed = (
        P(None, "vpair", "rank"),
        P("vpair", "rank"),
        P("vpair", "rank"),
        P(None, "vpair", None),
        P(),
        P(),
    )
    return jax.shard_map(
        shards, mesh=mesh, in_specs=placed, out_specs=(P(None, "vpair", None), P()), check_vma=False
    )
```

profile of v0, /device:TPU:0, one launch (start us, length us, event | category | flops | bytes accessed | tf_op | source)
XLA Modules:
  0.0 988.1 jit_solution(17243260461475593939)
XLA Ops:
  7.2 0.0 all-gather.6.cloned.1.call-start
  7.2 0.7 all-gather.6.cloned.1.call-update
  7.9 0.0 all-gather.12.cloned.1.call-start
  7.9 58.1 %all-gather.6.cloned.1.call-done = bf16[300,8192]{1,0:T(8,128)(2,1)} async-done(((bf16[300,1024]{1,0:T(8,128)(2,1)}), bf16[300,8192]{1,0:T(8,128)(2,1)}) %all-gather.6.cloned.1.call-update) | async-done | bytes 4915216 | tf_op jit(solution)/shard_map/all_gather | solution.py:16
  66.1 0.0 all-gather.12.cloned.1.call-update
  66.1 0.0 all-gather.8.cloned.1.call-start
  66.2 0.7 all-gather.8.cloned.1.call-update
  66.8 6.6 copy.34
  73.4 5.2 all-to-all-start
  78.6 213.5 %all-gather.12.cloned.1.call-done = bf16[4,300,8192]{2,1,0:T(8,128)(2,1)} async-done(((bf16[1,300,8192]{2,1,0:T(8,128)(2,1)}), bf16[4,300,8192]{2,1,0:T(8,128)(2,1)}) %all-gather.12.cloned.1.call-update) | async-done | bytes 19660816 | tf_op jit(solution)/shard_map/all_gather | solution.py:17
  292.1 20.4 %reshape.49 = bf16[1200,8192]{1,0:T(8,128)(2,1)} reshape(bf16[4,300,8192]{2,1,0:T(8,128)(2,1)} %all-gather.12.cloned.1.call-done) | data formatting | bytes 39321600
  312.5 54.9 %all-gather.8.cloned.1.call-done = bf16[8,300,1200]{1,0,2:T(8,128)(2,1)} async-done(((bf16[8,300,150]{1,0,2:T(8,128)(2,1)}), bf16[8,300,1200]{1,0,2:T(8,128)(2,1)}) %all-gather.8.cloned.1.call-update) | async-done | bytes 5760016 | tf_op jit(solution)/shard_map/all_gather | solution.py:23
  367.5 12.2 %convert_bitcast_fusion.1 = bf16[8,300,1024]{2,1,0:T(8,128)(2,1)} fusion(bf16[8,300,1200]{1,0,2:T(8,128)(2,1)} %all-gather.8.cloned.1.call-done, bf16[1200,8192]{1,0:T(8,128)(2,1)} %reshape.49, s32[]{:T(128)S(6)} %select_n.11), kind=kOutput, calls=%fused_computation.9 | convolution fusion | flops 5900697600 | bytes 14745604 | tf_op jit(solution)/shard_map/ons,sh->onh/dot_general | solution.py:21
  379.7 8.6 copy.38
  388.3 0.0 all-to-all-done
  388.3 5.2 all-to-all-start.1
  393.6 0.3 reduce-scatter.2.cloned.1.call-start
  393.9 6.7 convert_bitcast_fusion
  400.6 8.7 copy.35
  409.3 8.9 copy.36
  418.2 19.5 %reshape.51 = bf16[1200,8192,1]{1,0,2:T(8,128)(2,1)} reshape(bf16[4,300,8192]{2,1,0:T(8,128)(2,1)} %all-gather.12.cloned.1.call-done) | data formatting | bytes 39321600
  437.7 26.5 %all-to-all-done.1 = bf16[8,300,1024]{1,0,2:T(8,128)(2,1)} async-done(((bf16[8,300,1024]{1,0,2:T(8,128)(2,1)}), bf16[8,300,1024]{1,0,2:T(8,128)(2,1)}, u32[]{:S(2)}, u32[]{:S(2)}) %all-to-all-start.1) | async-done | bytes 4915232 | tf_op jit(solution)/shard_map/all_to_all | solution.py:33
  464.1 12.8 %copy.51 = bf16[8,300,4,256]{3,2,0,1:T(4,128)(2,1)} copy(bf16[8,300,4,256]{1,0,3,2:T(8,128)(2,1)} %bitcast.6) | data formatting | bytes 9830400 | tf_op jit(solution)/shard_map/all_to_all | solution.py:33
  476.9 5.2 copy.40
  482.2 54.1 %fusion.39 = bf16[8,8192,256]{1,2,0:T(8,128)(2,1)} fusion(f32[8192,256]{0,1:T(8,128)} %copy.36, bf16[1200,8192,1]{1,0,2:T(8,128)(2,1)} %reshape.51, bf16[8,1200,256]{2,0,1:T(8,128)(2,1)} %bitcast.49), kind=kOutput, calls=%fused_computation.1.clone.clone.clone.clone.clone.clone.1 | convolution fusion | flops 40298872832 | bytes 66519040 | tf_op jit(solution)/shard_map/cp,icq->ipq/dot_general | solution.py:30
  536.2 51.8 %fusion.13 = bf16[8,1200,256]{2,1,0:T(8,128)(2,1)} fusion(bf16[1200,8192,1]{1,0,2:T(8,128)(2,1)} %reshape.51, bf16[8,8192,256]{1,2,0:T(8,128)(2,1)} %fusion.39), kind=kOutput, calls=%fused_computation.11 | convolution fusion | flops 40267776000 | bytes 58130432 | tf_op jit(solution)/shard_map/ap,ipq->iaq/dot_general | solution.py:37
  588.0 8.8 copy.43
  596.8 58.1 %all_to_all.49 = bf16[8,1200,256]{2,0,1:T(8,128)(2,1)S(1)} all-to-all(bf16[8,1200,256]{2,0,1:T(8,128)(2,1)S(1)} %copy.43), channel_id=1, replica_groups=mesh['vpair'=4,'rank'=8] {'vpair'}, dimensions={1} | all-to-all | bytes 9830400 | tf_op jit(solution)/shard_map/all_to_all | solution.py:40
  654.9 0.7 copy.55
  655.6 10.7 %fusion.20 = f32[8,300,1200]{2,0,1:T(8,128)} fusion(bf16[8,300,1024]{2,0,1:T(8,128)(2,1)S(1)} %bitcast.48, bf16[1200,8192]{1,0:T(8,128)(2,1)} %reshape.49, s32[]{:T(128)S(6)} %select_n.11), kind=kOutput, calls=%fused_computation.12 | convolution fusion | flops 5898240000 | bytes 18892804 | tf_op jit(solution)/shard_map/iaq,bq->iab/dot_general | solution.py:41
  666.3 14.2 %copy.46 = f32[8,300,1200]{1,0,2:T(8,128)} copy(f32[8,300,1200]{2,0,1:T(8,128)} %fusion.20) | data formatting | bytes 23040000 | tf_op jit(solution)/shard_map/iaq,bq->iab/dot_general | solution.py:41
  680.5 0.0 reduce-scatter.2.cloned.1.call-update
  680.5 0.0 copy-start
  680.5 0.0 all-gather.10.cloned.1.call-start
  680.6 0.8 dynamic_slice.15
  681.3 0.8 dynamic_slice.14
  682.1 3.5 constant_dynamic-slice_fusion
  685.6 1.9 copy.54
  687.5 0.1 broadcast_add_fusion
  687.6 139.6 %reduce-scatter.2.cloned.1.call-done = f32[8,300,150]{1,0,2:T(8,128)} async-done(((f32[8,300,1200]{1,0,2:T(8,128)}), f32[8,300,150]{1,0,2:T(8,128)}) %reduce-scatter.2.cloned.1.call-update) | async-done | bytes 1440016 | tf_op jit(solution)/shard_map/reduce_scatter | solution.py:47
  827.1 0.0 copy-done
  827.1 4.3 multiply_reduce_fusion
  831.4 0.0 all-gather.10.cloned.1.call-update
  831.5 43.4 %psum.7 = f32[]{:T(128)} all-reduce(f32[]{:T(128)} %get-tuple-element.10), channel_id=1, replica_groups=mesh['vpair'=4,'rank'=8] {'vpair','rank'}, use_global_device_ids=true, to_apply=%region_2.0 | all-reduce | flops 1 | bytes 8 | tf_op jit(solution)/shard_map/psum | solution.py:54
  875.5 90.0 %all-gather.10.cloned.1.call-done = f32[8,300,1200]{1,0,2:T(8,128)} async-done(((f32[8,300,150]{1,0,2:T(8,128)}), f32[8,300,1200]{1,0,2:T(8,128)}) %all-gather.10.cloned.1.call-update) | async-done | bytes 11520016 | tf_op jit(solution)/shard_map/all_gather | solution.py:55
  965.5 14.7 %copy.47 = f32[8,300,1200]{2,0,1:T(8,128)} copy(f32[8,300,1200]{1,0,2:T(8,128)} %all-gather.10.cloned.1.call-done) | data formatting | bytes 23040000
Async XLA Ops:
  7.2 58.9 %all-gather.6.cloned.1.call-start = ((), (), s32[]{:S(2)}) async-start(), calls=%async_computation.4 | async-start | bytes 5603328 | tf_op jit(solution)/shard_map/all_gather | solution.py:16
  7.9 284.2 %all-gather.12.cloned.1.call-start = ((), (), s32[]{:S(2)}) async-start(), calls=%async_computation.8 | async-start | bytes 24903680 | tf_op jit(solution)/shard_map/all_gather | solution.py:17
  66.1 301.4 %all-gather.8.cloned.1.call-start = ((), (), s32[]{:S(2)}) async-start(), calls=%async_computation.5 | async-start | bytes 8294400 | tf_op jit(solution)/shard_map/all_gather | solution.py:23
  73.4 314.9 %all-to-all-start = ((bf16[2048,4,256]{0,2,1:T(8,128)(2,1)}), bf16[2048,4,256]{0,2,1:T(8,128)(2,1)}, u32[]{:S(2)}, u32[]{:S(2)}) async-start(bf16[2048,4,256]{0,2,1:T(8,128)(2,1)} %bitcast.46), calls=%async_computation | async-start | bytes 8388608 | tf_op jit(solution)/shard_map/all_to_all | solution.py:27
  388.3 75.8 %all-to-all-start.1 = ((bf16[8,300,1024]{1,0,2:T(8,128)(2,1)}), bf16[8,300,1024]{1,0,2:T(8,128)(2,1)}, u32[]{:S(2)}, u32[]{:S(2)}) async-start(bf16[8,300,1024]{1,0,2:T(8,128)(2,1)} %copy.38), calls=%async_computation.1 | async-start | bytes 12582912 | tf_op jit(solution)/shard_map/all_to_all | solution.py:33
  393.6 433.6 %reduce-scatter.2.cloned.1.call-start = ((), (), s32[]{:S(2)}) async-start(), calls=%async_computation.6 | async-start | bytes 16588800 | tf_op jit(solution)/shard_map/reduce_scatter | solution.py:47
  680.5 146.6 %copy-start = (f32[8]{0:T(128)S(1)}, f32[8]{0:T(128)}, u32[]{:S(2)}) copy-start(f32[8]{0:T(128)} %param.11) | copy-start | bytes 100
  680.5 285.0 %all-gather.10.cloned.1.call-start = ((), (), s32[]{:S(2)}) async-start(), calls=%async_computation.7 | async-start | bytes 16588800 | tf_op jit(solution)/shard_map/all_gather | solution.py:55
Sparse Core Ops, SparseCore 0:
  9.6 56.4 all-gather.5
  67.9 224.1 all-gather.11
  293.8 73.6 all-gather.7
  680.6 146.4 reduce-scatter.1
  831.6 133.8 all-gather.9
where the time goes:
time: 995 us; the launch traced here: 988 us
  waiting for transfers between devices  584 us (59%)
  local copies, waits for them, and re-layouts  136 us (14%)
  matrix products  129 us (13%)
  blocking collectives  102 us (10%)
  between operations  15.9 us (2%)
  other arithmetic  11 us (1%)
  starting transfers between devices  10.9 us (1%)
    all_gather x1, waiting for transfers between devices, shards(): factor_full = lax.all_gather(factor_rows, 'vpair', axis=0, tiled=True)  214 us
    reduce_scatter x1, waiting for transfers between devices, shards(): lax.psum_scatter(partial_value, 'rank', scatter_dimension=2, tiled=True)  140 us
    all_gather x1, waiting for transfers between devices, shards(): residual = lax.all_gather(part_residual, 'rank', axis=2, tiled=True)  90 us
    unnamed x7, local copies, waits for them, and re-layouts  63 us
    all_gather x1, waiting for transfers between devices, shards(): factor_rows = lax.all_gather(factors, 'rank', axis=1, tiled=True)  58.1 us
    all_to_all x1, blocking collectives, shards(): lax.all_to_all(ladder_half, 'vpair', split_axis=1, concat_axis=2, tiled=T...  58.1 us
    all_gather x1, waiting for transfers between devices, shards(): lax.all_gather(amplitudes, 'rank', axis=2, tiled=True)  54.9 us
    dot_general x1, matrix products, shards(): jnp.einsum('cp,icq->ipq', factor_full, lax.all_to_all(half_done, 'vpair',...  54.1 us
  transfers between devices with their start and end apart: 7, of which 6 were waited for; matrix products, arithmetic and copies ran while one was open for 10% of the time, Pallas kernels for 0%

commit v1 on v0

--- a/solution.py
+++ b/solution.py
@@ -4,6 +4,18 @@
 from jax.sharding import PartitionSpec as P
 
 epsilon = 1e-06
+
+
+def product_in_turn(x, axis, dim, product):
+    size, index = (lax.axis_size(axis), lax.axis_index(axis))
+    behind = [(i, (i - 1) % size) for i in range(size)]
+    rows = x.shape[dim]
+    current = x
+    total = product(current, index * rows)
+    for turn in range(1, size):
+        current = lax.ppermute(current, axis, behind)
+        total = total + product(current, (index + turn) % size * rows)
+    return total
 
 
 def shards(amplitudes, factors, kernel, other_terms, virt_energy, pair_energy):
@@ -18,11 +30,16 @@
     factor_cols = lax.dynamic_slice_in_dim(
         factor_full, lax.axis_index("rank") * right_block, right_block, 1
     )
-    half_done = jnp.einsum(
-        "ons,sh->onh",
-        lax.all_gather(amplitudes, "rank", axis=2, tiled=True),
-        factor_cols,
-        preferred_element_type=jnp.float32,
+    half_done = product_in_turn(
+        amplitudes,
+        "rank",
+        2,
+        lambda part, start: jnp.einsum(
+            "ons,sh->onh",
+            part,
+            lax.dynamic_slice_in_dim(factor_cols, start, part.shape[2], axis=0),
+            preferred_element_type=jnp.float32,
+        ),
     ).astype(jnp.bfloat16)
     kernel_sub = lax.all_to_all(kernel, "vpair", split_axis=1, concat_axis=0, tiled=True).astype(
         jnp.float32

time: 995 us -> 995 us (level)
  waiting for transfers between devices: 584 us -> 511 us
  matrix products: 129 us -> 181 us
  starting transfers between devices: 10.9 us -> 32.9 us
    all_gather x1, waiting for transfers between devices: 214 us -> 139 us  [shards(): factor_full = lax.all_gather(factor_rows, 'vpair', axis=0, tiled=True)]
    ppermute x0 -> x7, waiting for transfers between devices: none -> 55.1 us  [product_in_turn(): current = lax.ppermute(current, axis, behind)]
    all_gather x1 -> x0, waiting for transfers between devices: 54.9 us -> none  [shards(): lax.all_gather(amplitudes, 'rank', axis=2, tiled=True)]
    dot_general x1 -> x8, matrix products: 12.2 us -> 64.7 us  [shards(): jnp.einsum('ons,sh->onh', part, lax.dynamic_slice_in_dim(factor_cols, sta...]
    ppermute x0 -> x7, starting transfers between devices: none -> 22.2 us  [product_in_turn(): current = lax.ppermute(current, axis, behind)]
    unnamed x7 -> x17, local copies, waits for them, and re-layouts: 63 us -> 64.8 us
  transfers between devices with their start and end apart: 7 -> 13, of which waited for: 6 -> 10; matrix products, arithmetic and copies ran while one was open for 10% -> 15% of each run, Pallas kernels for 0% -> 0%
where the time goes in v1:
time: 995 us; the launch traced here: 990 us
  waiting for transfers between devices  511 us (51%)
  matrix products  181 us (18%)
  local copies, waits for them, and re-layouts  137 us (14%)
  blocking collectives  101 us (10%)
  starting transfers between devices  32.9 us (3%)
  between operations  16 us (2%)
  other arithmetic  11 us (1%)
    reduce_scatter x1, waiting for transfers between devices, shards(): lax.psum_scatter(partial_value, 'rank', scatter_dimension=2, tiled=True)  143 us
    all_gather x1, waiting for transfers between devices, shards(): factor_full = lax.all_gather(factor_rows, 'vpair', axis=0, tiled=True)  139 us
    all_gather x1, waiting for transfers between devices, shards(): residual = lax.all_gather(part_residual, 'rank', axis=2, tiled=True)  90 us
    unnamed x17, local copies, waits for them, and re-layouts  64.8 us
    dot_general x8, matrix products, shards(): jnp.einsum('ons,sh->onh', part, lax.dynamic_slice_in_dim(factor_cols, sta...  64.7 us
    all_gather x1, waiting for transfers between devices, shards(): factor_rows = lax.all_gather(factors, 'rank', axis=1, tiled=True)  58.1 us
    all_to_all x1, blocking collectives, shards(): lax.all_to_all(ladder_half, 'vpair', split_axis=1, concat_axis=2, tiled=T...  57.8 us
    ppermute x7, waiting for transfers between devices, product_in_turn(): current = lax.ppermute(current, axis, behind)  55.1 us
  transfers between devices with their start and end apart: 13, of which 10 were waited for; matrix products, arithmetic and copies ran while one was open for 15% of the time, Pallas kernels for 0%

profile of v1, /device:TPU:0, one launch (start us, length us, event | category | flops | bytes accessed | tf_op | source)
XLA Modules:
  0.0 990.0 jit_solution(16813119738426380797)
XLA Ops:
  7.9 58.1 %all-gather.5.cloned.1.call-done = bf16[300,8192]{1,0:T(8,128)(2,1)} async-done(((bf16[300,1024]{1,0:T(8,128)(2,1)}), bf16[300,8192]{1,0:T(8,128)(2,1)}) %all-gather.5.cloned.1.call-update) | async-done | bytes 4915216 | tf_op jit(solution)/shard_map/all_gather | solution.py:28
  66.9 11.3 %collective-permute-done = bf16[8,300,150]{1,0,2:T(8,128)(2,1)S(1)} collective-permute-done((bf16[8,300,150]{1,0,2:T(8,128)(2,1)}, bf16[8,300,150]{1,0,2:T(8,128)(2,1)S(1)}, u32[]{:S(2)}, u32[]{:S(2)}) %collective-permute-start) | collective-permute-done | bytes 720032 | tf_op jit(solution)/shard_map/ppermute | solution.py:16
  78.2 3.6 collective-permute-start.1
  81.8 11.0 %collective-permute-done.1 = bf16[8,300,150]{1,0,2:T(8,128)(2,1)S(1)} collective-permute-done((bf16[8,300,150]{1,0,2:T(8,128)(2,1)S(1)}, bf16[8,300,150]{1,0,2:T(8,128)(2,1)S(1)}, u32[]{:S(2)}, u32[]{:S(2)}) %collective-permute-start.1) | collective-permute-done | bytes 720032 | tf_op jit(solution)/shard_map/ppermute | solution.py:16
  92.8 3.7 collective-permute-start.2
  96.5 11.0 %collective-permute-done.2 = bf16[8,300,150]{1,0,2:T(8,128)(2,1)S(1)} collective-permute-done((bf16[8,300,150]{1,0,2:T(8,128)(2,1)S(1)}, bf16[8,300,150]{1,0,2:T(8,128)(2,1)S(1)}, u32[]{:S(2)}, u32[]{:S(2)}) %collective-permute-start.2) | collective-permute-done | bytes 720032 | tf_op jit(solution)/shard_map/ppermute | solution.py:16
  107.4 1.0 copy-done.1
  108.4 3.7 collective-permute-start.3
  112.1 11.0 %collective-permute-done.3 = bf16[8,300,150]{1,0,2:T(8,128)(2,1)S(1)} collective-permute-done((bf16[8,300,150]{1,0,2:T(8,128)(2,1)S(1)}, bf16[8,300,150]{1,0,2:T(8,128)(2,1)S(1)}, u32[]{:S(2)}, u32[]{:S(2)}) %collective-permute-start.3) | collective-permute-done | bytes 720032 | tf_op jit(solution)/shard_map/ppermute | solution.py:16
  123.1 0.9 copy-done.3
  124.0 3.7 collective-permute-start.4
  127.7 11.0 %collective-permute-done.4 = bf16[8,300,150]{1,0,2:T(8,128)(2,1)} collective-permute-done((bf16[8,300,150]{1,0,2:T(8,128)(2,1)S(1)}, bf16[8,300,150]{1,0,2:T(8,128)(2,1)}, u32[]{:S(2)}, u32[]{:S(2)}) %collective-permute-start.4) | collective-permute-done | bytes 720032 | tf_op jit(solution)/shard_map/ppermute | solution.py:16
  138.6 3.8 collective-permute-start.5
  142.5 7.1 copy.37
  149.5 4.9 all-to-all-start
  154.5 2.9 collective-permute-start.6
  157.4 138.6 %all-gather.9.cloned.1.call-done = bf16[4,300,8192]{2,1,0:T(8,128)(2,1)} async-done(((bf16[1,300,8192]{2,1,0:T(8,128)(2,1)}), bf16[4,300,8192]{2,1,0:T(8,128)(2,1)}) %all-gather.9.cloned.1.call-update) | async-done | bytes 19660816 | tf_op jit(solution)/shard_map/all_gather | solution.py:29
  296.0 19.7 %reshape.49 = bf16[1200,8192]{1,0:T(8,128)(2,1)} reshape(bf16[4,300,8192]{2,1,0:T(8,128)(2,1)} %all-gather.9.cloned.1.call-done) | data formatting | bytes 39321600
  315.8 2.6 fusion.33
  318.4 6.8 fusion.21
  325.2 6.8 fusion.23
  332.0 6.4 fusion.25
  338.3 6.4 fusion.27
  344.8 6.4 fusion.29
  351.1 6.3 fusion.31
  357.5 23.0 %fusion.9 = bf16[8,300,1024]{2,1,0:T(8,128)(2,1)} fusion(f32[1024,8,300]{0,2,1:T(8,128)} %fusion.21, f32[1024,8,300]{0,2,1:T(8,128)} %fusion.23, f32[1024,8,300]{0,2,1:T(8,128)} %fusion.25, f32[1024,8,300]{0,2,1:T(8,128)} %fusion.27, f32[1024,8,300]{0,2,1:T(8,128)} %fusion.29, f32[1024,8,300]{0,2,1:T(8,128)S(1)} %fusion.33, f32[1024,8,300]{0,2,1:T(8,128)} %fusion.31, ...), kind=kOutput, calls=%fused_computation.8 | convolution fusion | flops 756940800 | bytes 75747336 | tf_op jit(solution)/shard_map/ons,sh->onh/dot_general | solution.py:37
  380.5 8.6 copy.48
  389.0 5.6 all-to-all-start.1
  394.7 6.7 convert_bitcast_fusion
  401.4 8.7 copy.38
  410.1 8.9 copy.39
  419.0 19.5 %reshape.58 = bf16[1200,8192,1]{1,0,2:T(8,128)(2,1)} reshape(bf16[4,300,8192]{2,1,0:T(8,128)(2,1)} %all-gather.9.cloned.1.call-done) | data formatting | bytes 39321600
  438.4 26.2 %all-to-all-done.1 = bf16[8,300,1024]{1,0,2:T(8,128)(2,1)} async-done(((bf16[8,300,1024]{1,0,2:T(8,128)(2,1)}), bf16[8,300,1024]{1,0,2:T(8,128)(2,1)}, u32[]{:S(2)}, u32[]{:S(2)}) %all-to-all-start.1) | async-done | bytes 4915232 | tf_op jit(solution)/shard_map/all_to_all | solution.py:50
  464.7 12.8 %copy.61 = bf16[8,300,4,256]{3,2,0,1:T(4,128)(2,1)} copy(bf16[8,300,4,256]{1,0,3,2:T(8,128)(2,1)} %bitcast.13) | data formatting | bytes 9830400 | tf_op jit(solution)/shard_map/all_to_all | solution.py:50
  477.5 5.2 copy.50
  482.7 53.5 %fusion.64 = bf16[8,8192,256]{1,2,0:T(8,128)(2,1)} fusion(f32[8192,256]{0,1:T(8,128)} %copy.39, bf16[1200,8192,1]{1,0,2:T(8,128)(2,1)} %reshape.58, bf16[8,1200,256]{2,0,1:T(8,128)(2,1)} %bitcast.71), kind=kOutput, calls=%fused_computation.1.clone.clone.clone.clone.clone.clone.1 | convolution fusion | flops 40298872832 | bytes 66519040 | tf_op jit(solution)/shard_map/cp,icq->ipq/dot_general | solution.py:47
  536.2 51.8 %fusion.12 = bf16[8,1200,256]{2,1,0:T(8,128)(2,1)} fusion(bf16[1200,8192,1]{1,0,2:T(8,128)(2,1)} %reshape.58, bf16[8,8192,256]{1,2,0:T(8,128)(2,1)} %fusion.64), kind=kOutput, calls=%fused_computation.10 | convolution fusion | flops 40267776000 | bytes 58130432 | tf_op jit(solution)/shard_map/ap,ipq->iaq/dot_general | solution.py:54
  587.9 8.8 copy.53
  596.8 57.8 %all_to_all.49 = bf16[8,1200,256]{2,0,1:T(8,128)(2,1)S(1)} all-to-all(bf16[8,1200,256]{2,0,1:T(8,128)(2,1)S(1)} %copy.53), channel_id=1, replica_groups=mesh['vpair'=4,'rank'=8] {'vpair'}, dimensions={1} | all-to-all | bytes 9830400 | tf_op jit(solution)/shard_map/all_to_all | solution.py:57
  655.3 10.7 %fusion.17 = f32[8,300,1200]{2,0,1:T(8,128)} fusion(bf16[8,300,1024]{2,0,1:T(8,128)(2,1)S(1)} %bitcast.70, bf16[1200,8192]{1,0:T(8,128)(2,1)} %reshape.49, s32[]{:T(128)S(6)} %select_n.83), kind=kOutput, calls=%fused_computation.11 | convolution fusion | flops 5898240000 | bytes 18892804 | tf_op jit(solution)/shard_map/iaq,bq->iab/dot_general | solution.py:58
  666.0 14.2 %copy.56 = f32[8,300,1200]{1,0,2:T(8,128)} copy(f32[8,300,1200]{2,0,1:T(8,128)} %fusion.17) | data formatting | bytes 23040000 | tf_op jit(solution)/shard_map/iaq,bq->iab/dot_general | solution.py:58
  681.8 2.7 constant_dynamic-slice_fusion
  684.5 1.9 copy.64
  686.5 142.5 %reduce-scatter.2.cloned.1.call-done = f32[8,300,150]{1,0,2:T(8,128)} async-done(((f32[8,300,1200]{1,0,2:T(8,128)}), f32[8,300,150]{1,0,2:T(8,128)}) %reduce-scatter.2.cloned.1.call-update) | async-done | bytes 1440016 | tf_op jit(solution)/shard_map/reduce_scatter | solution.py:64
  829.0 4.3 multiply_reduce_fusion
  833.4 43.4 %psum.7 = f32[]{:T(128)} all-reduce(f32[]{:T(128)} %get-tuple-element.10), channel_id=1, replica_groups=mesh['vpair'=4,'rank'=8] {'vpair','rank'}, use_global_device_ids=true, to_apply=%region_2.3 | all-reduce | flops 1 | bytes 8 | tf_op jit(solution)/shard_map/psum | solution.py:71
  877.4 90.0 %all-gather.7.cloned.1.call-done = f32[8,300,1200]{1,0,2:T(8,128)} async-done(((f32[8,300,150]{1,0,2:T(8,128)}), f32[8,300,1200]{1,0,2:T(8,128)}) %all-gather.7.cloned.1.call-update) | async-done | bytes 11520016 | tf_op jit(solution)/shard_map/all_gather | solution.py:72
  967.4 14.7 %copy.57 = f32[8,300,1200]{2,0,1:T(8,128)} copy(f32[8,300,1200]{1,0,2:T(8,128)} %all-gather.7.cloned.1.call-done) | data formatting | bytes 23040000
  (26 shorter events, 4.1 us)
Async XLA Ops:
  7.2 58.9 %all-gather.5.cloned.1.call-start = ((), (), s32[]{:S(2)}) async-start(), calls=%async_computation.4 | async-start | bytes 5603328 | tf_op jit(solution)/shard_map/all_gather | solution.py:28
  7.9 288.1 %all-gather.9.cloned.1.call-start = ((), (), s32[]{:S(2)}) async-start(), calls=%async_computation.7 | async-start | bytes 24903680 | tf_op jit(solution)/shard_map/all_gather | solution.py:29
  66.1 12.1 %collective-permute-start = (bf16[8,300,150]{1,0,2:T(8,128)(2,1)}, bf16[8,300,150]{1,0,2:T(8,128)(2,1)S(1)}, u32[]{:S(2)}, u32[]{:S(2)}) collective-permute-start(bf16[8,300,150]{1,0,2:T(8,128)(2,1)} %param.6), channel_id=1, source_target_pairs={{0,7},{1,0},{2,1},{3,2},{4,3},{5,4},{6,5},{7,6},{8,15},{9,8},{10,9... | collective-permute-start | bytes 2160008 | tf_op jit(solution)/shard_map/ppermute | solution.py:16
  78.2 14.6 %collective-permute-start.1 = (bf16[8,300,150]{1,0,2:T(8,128)(2,1)S(1)}, bf16[8,300,150]{1,0,2:T(8,128)(2,1)S(1)}, u32[]{:S(2)}, u32[]{:S(2)}) collective-permute-start(bf16[8,300,150]{1,0,2:T(8,128)(2,1)S(1)} %collective-permute-done), channel_id=1, source_target_pairs={{0,7},{1,0},{2,1},{3,2},{4,3},{5,4},{6,5},{7,6},{8,15},{9,8},{10,9... | collective-permute-start | bytes 2160008 | tf_op jit(solution)/shard_map/ppermute | solution.py:16
  92.8 14.7 %collective-permute-start.2 = (bf16[8,300,150]{1,0,2:T(8,128)(2,1)S(1)}, bf16[8,300,150]{1,0,2:T(8,128)(2,1)S(1)}, u32[]{:S(2)}, u32[]{:S(2)}) collective-permute-start(bf16[8,300,150]{1,0,2:T(8,128)(2,1)S(1)} %collective-permute-done.1), channel_id=1, source_target_pairs={{0,7},{1,0},{2,1},{3,2},{4,3},{5,4},{6,5},{7,6},{8,15},{9,8},{10,9... | collective-permute-start | bytes 2160008 | tf_op jit(solution)/shard_map/ppermute | solution.py:16
  107.4 1.0 copy-start.1
  108.4 14.7 %collective-permute-start.3 = (bf16[8,300,150]{1,0,2:T(8,128)(2,1)S(1)}, bf16[8,300,150]{1,0,2:T(8,128)(2,1)S(1)}, u32[]{:S(2)}, u32[]{:S(2)}) collective-permute-start(bf16[8,300,150]{1,0,2:T(8,128)(2,1)S(1)} %collective-permute-done.2), channel_id=1, source_target_pairs={{0,7},{1,0},{2,1},{3,2},{4,3},{5,4},{6,5},{7,6},{8,15},{9,8},{10,9... | collective-permute-start | bytes 2160008 | tf_op jit(solution)/shard_map/ppermute | solution.py:16
  123.1 0.9 copy-start.3
  124.0 14.7 %collective-permute-start.4 = (bf16[8,300,150]{1,0,2:T(8,128)(2,1)S(1)}, bf16[8,300,150]{1,0,2:T(8,128)(2,1)}, u32[]{:S(2)}, u32[]{:S(2)}) collective-permute-start(bf16[8,300,150]{1,0,2:T(8,128)(2,1)S(1)} %collective-permute-done.3), channel_id=1, source_target_pairs={{0,7},{1,0},{2,1},{3,2},{4,3},{5,4},{6,5},{7,6},{8,15},{9,8},{10,9... | collective-permute-start | bytes 2160008 | tf_op jit(solution)/shard_map/ppermute | solution.py:16
  138.6 15.9 %collective-permute-start.5 = (bf16[8,300,150]{1,0,2:T(8,128)(2,1)}, bf16[8,300,150]{1,0,2:T(8,128)(2,1)}, u32[]{:S(2)}, u32[]{:S(2)}) collective-permute-start(bf16[8,300,150]{1,0,2:T(8,128)(2,1)} %collective-permute-done.4), channel_id=1, source_target_pairs={{0,7},{1,0},{2,1},{3,2},{4,3},{5,4},{6,5},{7,6},{8,15},{9,8},{10,9... | collective-permute-start | bytes 2160008 | tf_op jit(solution)/shard_map/ppermute | solution.py:16
  149.5 239.5 %all-to-all-start = ((bf16[2048,4,256]{0,2,1:T(8,128)(2,1)}), bf16[2048,4,256]{0,2,1:T(8,128)(2,1)}, u32[]{:S(2)}, u32[]{:S(2)}) async-start(bf16[2048,4,256]{0,2,1:T(8,128)(2,1)} %bitcast.68), calls=%async_computation | async-start | bytes 8388608 | tf_op jit(solution)/shard_map/all_to_all | solution.py:44
  154.5 161.3 %copy-start = (bf16[8,300,150]{1,0,2:T(8,128)(2,1)S(1)}, bf16[8,300,150]{1,0,2:T(8,128)(2,1)}, u32[]{:S(2)}) copy-start(bf16[8,300,150]{1,0,2:T(8,128)(2,1)} %param.6) | copy-start | bytes 2160004
  154.5 203.0 %collective-permute-start.6 = (bf16[8,300,150]{1,0,2:T(8,128)(2,1)}, bf16[8,300,150]{1,0,2:T(8,128)(2,1)}, u32[]{:S(2)}, u32[]{:S(2)}) collective-permute-start(bf16[8,300,150]{1,0,2:T(8,128)(2,1)} %collective-permute-done.5), channel_id=1, source_target_pairs={{0,7},{1,0},{2,1},{3,2},{4,3},{5,4},{6,5},{7,6},{8,15},{9,8},{10,9... | collective-permute-start | bytes 2160008 | tf_op jit(solution)/shard_map/ppermute | solution.py:16
  325.2 6.8 copy-start.4
  332.0 6.4 copy-start.2
  389.0 75.6 %all-to-all-start.1 = ((bf16[8,300,1024]{1,0,2:T(8,128)(2,1)}), bf16[8,300,1024]{1,0,2:T(8,128)(2,1)}, u32[]{:S(2)}, u32[]{:S(2)}) async-start(bf16[8,300,1024]{1,0,2:T(8,128)(2,1)} %copy.48), calls=%async_computation.1 | async-start | bytes 12582912 | tf_op jit(solution)/shard_map/all_to_all | solution.py:50
  394.7 434.4 %reduce-scatter.2.cloned.1.call-start = ((), (), s32[]{:S(2)}) async-start(), calls=%async_computation.5 | async-start | bytes 16588800 | tf_op jit(solution)/shard_map/reduce_scatter | solution.py:64
  680.2 148.9 %copy-start.5 = (f32[8]{0:T(128)S(1)}, f32[8]{0:T(128)}, u32[]{:S(2)}) copy-start(f32[8]{0:T(128)} %param.11) | copy-start | bytes 100
  680.2 287.3 %all-gather.7.cloned.1.call-start = ((), (), s32[]{:S(2)}) async-start(), calls=%async_computation.6 | async-start | bytes 16588800 | tf_op jit(solution)/shard_map/all_gather | solution.py:72
Sparse Core Ops, SparseCore 0:
  9.6 56.4 all-gather.4
  67.9 228.0 all-gather.8
  680.3 148.6 reduce-scatter.1
  833.5 133.9 all-gather.6
